TPU v7x, 32 devices: a whole 2x2x4 slice. The times are simulated.
32 devices in a mesh: section: 2 (over core), dp: 8 (over z, y), mp: 2 (over x).
Axes of the slice: x: 2, y: 2, z: 4, core: 2. Of those that a mesh axis runs over, the one named last changes fastest.
Arguments:
- hidden_in: bfloat16 [32, 512, 768], P('dp'), may hold values from -6 to 6
- segment_ids: int32 [32, 512], P('dp'), may hold values from 0 to 3, never falling along the last dimension, each value on 1 to 256 neighbouring positions
- cotangent: float32 [32, 512, 768], P('dp'), may hold values from -6 to 6
- w_proj: bfloat16 [2, 5, 768, 384], P('section', None, None, 'mp'), may hold values from -0.21875 to 0.21875
- w_depth: bfloat16 [2, 9, 768], P('section'), may hold values from -2 to 2
- w_kernel: bfloat16 [2, 384, 54], P('section', 'mp'), may hold values from -0.3125 to 0.3125
- w_out: bfloat16 [2, 2, 384, 768], P('section', None, 'mp'), may hold values from -0.625 to 0.625
- w_expand: bfloat16 [2, 2, 384, 1536], P('section', 'mp'), may hold values from -0.3125 to 0.3125
- shrink_weight: bfloat16 [2, 2, 1536, 384], P('section', 'mp'), may hold values from -0.21875 to 0.21875
- ln_gain: bfloat16 [2, 2, 768], P('section'), may hold values from 0.25 to 1.75
- ln_bias: bfloat16 [2, 2, 768], P('section'), may hold values from -3 to 3
Outputs:
- layer_outputs: bfloat16 [2, 32, 512, 768], P('section', 'dp')
- input_grads: float32 [2, 32, 512, 768], P('section', 'dp')
- proj_grad: float32 [2, 5, 768, 384], P('section', None, None, 'mp')
- depth_grad: float32 [2, 9, 768], P('section')
- kernel_grad: float32 [2, 384, 54], P('section', 'mp')
- out_grad: float32 [2, 2, 384, 768], P('section', None, 'mp')
- expand_grad: float32 [2, 2, 384, 1536], P('section', 'mp')
- shrink_grad: float32 [2, 2, 1536, 384], P('section', 'mp')
- gain_grad: float32 [2, 2, 768], P('section')
- bias_grad: float32 [2, 2, 768], P('section')
Inputs may be any that keep to these rules, and one draw needn't show every extreme that they name: `segment_ids`: along each row the ids never fall; each row holds 4 documents of 1 to 256 consecutive tokens, and some row has a document of exactly 256 tokens.
All inputs are finite; a program needn't handle non-finite values.
Results may differ from a plain program's by a relative error of at most 0.025.
Values may be sent and summed in bfloat16 or wider, within the bound.
A program may use at most 320 MiB of HBM per device.

v0:
```python
from functools import partial

import jax
import jax.numpy as jnp
from jax import lax
from jax.sharding import PartitionSpec as P

ATT_HEADS = 6
HEAD = 64
KSIZE = 9
MICRO = 4
MB_ROWS = 1


EPS = 1e-05
FLOOR = -1000000000.0


def from_behind(value, axis, by):
    peers = lax.axis_size(axis)
    pairs = [(i, i + by) for i in range(peers) if 0 <= i + by < peers]
    return lax.ppermute(value, axis, pairs)


def shifted_masks(segment, tap_count):
    half_width = tap_count // 2
    padded = jnp.pad(segment, ((0, 0), (half_width, half_width)), constant_values=-1)
    sequence_length = segment.shape[1]
    return [
        lax.slice_in_dim(padded, offset, offset + sequence_length, axis=1) == segment
        for offset in range(tap_count)
    ]


def expand_mask(tap_mask, target_rank):
    return tap_mask.reshape(tap_mask.shape + (1,) * (target_rank - 2))


def padded_rows(values, tap_count):
    half_width = tap_count // 2
    pad_spec = [(0, 0)] * values.ndim
    pad_spec[1] = (half_width, half_width)
    return jnp.pad(values, pad_spec)


def tap_take(values, tap_mask, offset, tap_count):
    window = lax.slice_in_dim(
        padded_rows(values, tap_count), offset, offset + values.shape[1], axis=1
    )
    return jnp.where(expand_mask(tap_mask, values.ndim), window, 0.0)


def tap_give(grad_vals, tap_mask, offset, tap_count):
    masked = jnp.where(expand_mask(tap_mask, grad_vals.ndim), grad_vals, 0.0)
    begin_at = tap_count - 1 - offset
    return lax.slice_in_dim(
        padded_rows(masked, tap_count), begin_at, begin_at + grad_vals.shape[1], axis=1
    )


def norm_forward(summed, gain_row, bias_row):
    centered = summed - jnp.mean(summed, axis=-1, keepdims=True)
    inverse = lax.rsqrt(jnp.mean(centered * centered, axis=-1, keepdims=True) + EPS)
    normed = centered * inverse
    return (normed * gain_row + bias_row, normed, inverse)


def norm_backward(grad_output, normed, inverse, gain_row):
    scaled = grad_output * gain_row
    grad_input = inverse * (
        scaled
        - jnp.mean(scaled, axis=-1, keepdims=True)
        - normed * jnp.mean(scaled * normed, axis=-1, keepdims=True)
    )
    return (
        grad_input,
        jnp.sum(grad_output * normed, axis=(0, 1)),
        jnp.sum(grad_output, axis=(0, 1)),
    )


def score_block(queries_low, keys_low, segment):
    scores = jnp.einsum(
        "bqhd,bkhd->bhqk", queries_low, keys_low, preferred_element_type=jnp.float32
    ) * HEAD ** (-0.5)
    same_doc = (segment[:, :, None] == segment[:, None, :])[:, None]
    return (jnp.where(same_doc, scores, FLOOR), same_doc)


def head_views(projected, heads_here):
    batch_row_count, sequence_length = (projected.shape[1], projected.shape[2])
    queries_low = (
        projected[0]
        .astype(jnp.bfloat16)
        .reshape(batch_row_count, sequence_length, heads_here, HEAD)
    )
    keys_low = (
        projected[1]
        .astype(jnp.bfloat16)
        .reshape(batch_row_count, sequence_length, heads_here, HEAD)
    )
    values_low = (
        projected[2]
        .astype(jnp.bfloat16)
        .reshape(batch_row_count, sequence_length, heads_here, HEAD)
    )
    return (queries_low, keys_low, values_low)


def layer_forward(inputs, segment, weights):
    w_proj, w_depth, w_kernel, w_out, w_expand, shrink_weight, norm_gains, norm_biases = weights
    batch_row_count, sequence_length, hidden_width = inputs.shape
    heads_here = ATT_HEADS // lax.axis_size("mp")
    local_width = heads_here * HEAD
    tap_masks = shifted_masks(segment, KSIZE)
    inputs_low = inputs.astype(jnp.bfloat16)
    projected = jnp.einsum(
        "bld,pda->pbla", inputs_low, w_proj[:4], preferred_element_type=jnp.float32
    )
    depth_conv = jnp.zeros(inputs.shape, jnp.float32)
    for tap_index in range(KSIZE):
        depth_conv = (
            depth_conv
            + tap_take(inputs, tap_masks[tap_index], tap_index, KSIZE) * w_depth[tap_index]
        )
    depth_low = depth_conv.astype(jnp.bfloat16)
    key_conv = jnp.einsum("bld,da->bla", depth_low, w_proj[4], preferred_element_type=jnp.float32)
    product_low = (key_conv * projected[0]).astype(jnp.bfloat16)
    logit_part = jnp.einsum(
        "bla,ak->blk", product_low, w_kernel, preferred_element_type=jnp.float32
    )
    logits = lax.psum_scatter(logit_part, "mp", scatter_dimension=2, tiled=True)
    kernel = jax.nn.softmax(
        logits.reshape(batch_row_count, sequence_length, heads_here, KSIZE), axis=-1
    )
    conv_value = projected[3].reshape(batch_row_count, sequence_length, heads_here, HEAD)
    conv_mixed = jnp.zeros(conv_value.shape, jnp.float32)
    for tap_index in range(KSIZE):
        conv_mixed = conv_mixed + kernel[..., tap_index, None] * tap_take(
            conv_value, tap_masks[tap_index], tap_index, KSIZE
        )
    queries_low, keys_low, values_low = head_views(projected, heads_here)
    masked, same_doc = score_block(queries_low, keys_low, segment)
    row_top = jnp.max(masked, axis=-1, keepdims=True)
    exp_scores = jnp.exp(masked - row_top)
    row_total = jnp.sum(exp_scores, axis=-1, keepdims=True)
    log_total = row_top + jnp.log(row_total)
    probs_low = (exp_scores / row_total).astype(jnp.bfloat16)
    context = jnp.einsum(
        "bhqk,bkhd->bqhd", probs_low, values_low, preferred_element_type=jnp.float32
    )
    stacked = jnp.stack(
        [
            context.reshape(batch_row_count, sequence_length, local_width),
            conv_mixed.reshape(batch_row_count, sequence_length, local_width),
        ]
    ).astype(jnp.bfloat16)
    mixer_part = jnp.einsum("pbla,pad->bld", stacked, w_out, preferred_element_type=jnp.float32)
    group_width = w_expand.shape[1]
    group_start = lax.axis_index("mp") * group_width
    mixer_out = lax.psum(mixer_part, "mp")
    first_out, normed_one, inverse_one = norm_forward(
        mixer_out + inputs, norm_gains[0], norm_biases[0]
    )
    group_low = lax.dynamic_slice_in_dim(first_out, group_start, group_width, 2).astype(
        jnp.bfloat16
    )
    hidden_pre = jnp.einsum(
        "blc,cf->blf", group_low, w_expand[0], preferred_element_type=jnp.float32
    )
    active_lower_half = jax.nn.gelu(hidden_pre, approximate=False).astype(jnp.bfloat16)
    group_out = jnp.einsum(
        "blf,fc->blc", active_lower_half, shrink_weight[0], preferred_element_type=jnp.float32
    )
    feedforward_output = lax.all_gather(
        group_out.astype(jnp.bfloat16), "mp", axis=2, tiled=True
    ).astype(group_out.dtype)
    second_out, normed_two, inverse_two = norm_forward(
        feedforward_output + first_out, norm_gains[1], norm_biases[1]
    )
    out_low = second_out.astype(jnp.bfloat16)
    kept_state = (
        inputs,
        projected,
        depth_low,
        key_conv,
        product_low,
        kernel,
        log_total,
        stacked,
        normed_one,
        inverse_one,
        group_low,
        hidden_pre,
        active_lower_half,
        normed_two,
        inverse_two,
    )
    return (out_low, kept_state)


def ffn_backward(grad_output, kept_state, weights):
    w_proj, w_depth, w_kernel, w_out, w_expand, shrink_weight, norm_gains, norm_biases = weights
    (
        inputs,
        projected,
        depth_low,
        key_conv,
        product_low,
        kernel,
        log_total,
        stacked,
        normed_one,
        inverse_one,
        group_low,
        hidden_pre,
        active_lower_half,
        normed_two,
        inverse_two,
    ) = kept_state
    group_width = w_expand.shape[1]
    group_start = lax.axis_index("mp") * group_width
    grad_sum_two, gain_part, bias_part = norm_backward(
        grad_output, normed_two, inverse_two, norm_gains[1]
    )
    grad_group_low = lax.dynamic_slice_in_dim(grad_sum_two, group_start, group_width, 2).astype(
        jnp.bfloat16
    )
    shrink_grad = jnp.einsum(
        "blf,blc->fc", active_lower_half, grad_group_low, preferred_element_type=jnp.float32
    )
    grad_active = jnp.einsum(
        "blc,fc->blf", grad_group_low, shrink_weight[0], preferred_element_type=jnp.float32
    )
    gelu_pull = jax.vjp(partial(jax.nn.gelu, approximate=False), hidden_pre)[1]
    grad_pre_low = gelu_pull(grad_active)[0].astype(jnp.bfloat16)
    expand_grad = jnp.einsum(
        "blc,blf->cf", group_low, grad_pre_low, preferred_element_type=jnp.float32
    )
    grad_group_in = jnp.einsum(
        "blf,cf->blc", grad_pre_low, w_expand[0], preferred_element_type=jnp.float32
    )
    grad_first = grad_sum_two + lax.all_gather(
        grad_group_in.astype(jnp.bfloat16), "mp", axis=2, tiled=True
    ).astype(grad_group_in.dtype)
    return (grad_first, (expand_grad[None, None], shrink_grad[None, None]), (gain_part, bias_part))


def mixer_backward(grad_first, segment, kept_state, weights, ffn_norm):
    w_proj, w_depth, w_kernel, w_out, w_expand, shrink_weight, norm_gains, norm_biases = weights
    (
        inputs,
        projected,
        depth_low,
        key_conv,
        product_low,
        kernel,
        log_total,
        stacked,
        normed_one,
        inverse_one,
        group_low,
        hidden_pre,
        active_lower_half,
        normed_two,
        inverse_two,
    ) = kept_state
    batch_row_count, sequence_length, hidden_width = inputs.shape
    heads_here = ATT_HEADS // lax.axis_size("mp")
    local_width = heads_here * HEAD
    tap_masks = shifted_masks(segment, KSIZE)
    inputs_low = inputs.astype(jnp.bfloat16)
    grad_sum_one, gain_one, bias_one = norm_backward(
        grad_first, normed_one, inverse_one, norm_gains[0]
    )
    grad_mixed_low = grad_sum_one.astype(jnp.bfloat16)
    out_grad = jnp.einsum(
        "pbla,bld->pad", stacked, grad_mixed_low, preferred_element_type=jnp.float32
    )
    grad_stacked = jnp.einsum(
        "bld,pad->pbla", grad_mixed_low, w_out, preferred_element_type=jnp.float32
    ).astype(jnp.bfloat16)
    grad_context = grad_stacked[0].reshape(batch_row_count, sequence_length, heads_here, HEAD)
    grad_conv = (
        grad_stacked[1]
        .astype(jnp.float32)
        .reshape(batch_row_count, sequence_length, heads_here, HEAD)
    )
    queries_low, keys_low, values_low = head_views(projected, heads_here)
    masked, same_doc = score_block(queries_low, keys_low, segment)
    attn_probs = jnp.exp(masked - log_total)
    probs_low = attn_probs.astype(jnp.bfloat16)
    grad_probs = jnp.einsum(
        "bqhd,bkhd->bhqk", grad_context, values_low, preferred_element_type=jnp.float32
    )
    row_dot = jnp.sum(attn_probs * grad_probs, axis=-1, keepdims=True)
    grad_scores = jnp.where(same_doc, attn_probs * (grad_probs - row_dot), 0.0).astype(jnp.bfloat16)
    score_scale = HEAD ** (-0.5)
    grad_queries = (
        jnp.einsum("bhqk,bkhd->bqhd", grad_scores, keys_low, preferred_element_type=jnp.float32)
        * score_scale
    )
    grad_keys = (
        jnp.einsum("bhqk,bqhd->bkhd", grad_scores, queries_low, preferred_element_type=jnp.float32)
        * score_scale
    )
    grad_values = jnp.einsum(
        "bhqk,bqhd->bkhd", probs_low, grad_context, preferred_element_type=jnp.float32
    )
    conv_value = projected[3].reshape(batch_row_count, sequence_length, heads_here, HEAD)
    kernel_taps = []
    grad_conv_value = jnp.zeros(conv_value.shape, jnp.float32)
    for tap_index in range(KSIZE):
        shifted = tap_take(conv_value, tap_masks[tap_index], tap_index, KSIZE)
        kernel_taps.append(jnp.sum(grad_conv * shifted, axis=-1))
        grad_conv_value = grad_conv_value + tap_give(
            kernel[..., tap_index, None] * grad_conv, tap_masks[tap_index], tap_index, KSIZE
        )
    grad_kernel = jnp.stack(kernel_taps, axis=-1)
    grad_logits = kernel * (grad_kernel - jnp.sum(kernel * grad_kernel, axis=-1, keepdims=True))
    grad_logits_low = grad_logits.reshape(
        batch_row_count, sequence_length, heads_here * KSIZE
    ).astype(jnp.bfloat16)
    grad_logits_all = lax.all_gather(grad_logits_low, "mp", axis=2, tiled=True)
    kernel_grad = jnp.einsum(
        "bla,blk->ak", product_low, grad_logits_all, preferred_element_type=jnp.float32
    )
    grad_product = jnp.einsum(
        "blk,ak->bla", grad_logits_all, w_kernel, preferred_element_type=jnp.float32
    )
    grad_key_conv = (grad_product * projected[0]).astype(jnp.bfloat16)
    grad_query = (
        grad_queries.reshape(batch_row_count, sequence_length, local_width)
        + grad_product * key_conv
    ).astype(jnp.bfloat16)
    point_grad = jnp.einsum(
        "bld,bla->da", depth_low, grad_key_conv, preferred_element_type=jnp.float32
    )
    grad_depth = jnp.einsum(
        "bla,da->bld", grad_key_conv, w_proj[4], preferred_element_type=jnp.float32
    )
    depth_grads = []
    grad_from_depth = jnp.zeros(inputs.shape, jnp.float32)
    for tap_index in range(KSIZE):
        depth_grads.append(
            jnp.sum(
                grad_depth * tap_take(inputs, tap_masks[tap_index], tap_index, KSIZE), axis=(0, 1)
            )
        )
        grad_from_depth = grad_from_depth + tap_give(
            grad_depth * w_depth[tap_index], tap_masks[tap_index], tap_index, KSIZE
        )
    depth_part = jnp.stack(depth_grads)
    grad_proj_low = jnp.stack(
        [
            grad_query,
            grad_keys.reshape(batch_row_count, sequence_length, local_width).astype(jnp.bfloat16),
            grad_values.reshape(batch_row_count, sequence_length, local_width).astype(jnp.bfloat16),
            grad_conv_value.reshape(batch_row_count, sequence_length, local_width).astype(
                jnp.bfloat16
            ),
        ]
    )
    proj_grad = jnp.concatenate(
        [
            jnp.einsum(
                "bld,pbla->pda", inputs_low, grad_proj_low, preferred_element_type=jnp.float32
            ),
            point_grad[None],
        ],
        axis=0,
    )
    grad_part = (
        jnp.einsum("pbla,pda->bld", grad_proj_low, w_proj[:4], preferred_element_type=jnp.float32)
        + grad_from_depth
    )
    gain_pair = jnp.stack([gain_one, ffn_norm[0]])
    bias_pair = jnp.stack([bias_one, ffn_norm[1]])
    grad_summed, depth_total = (
        lax.psum(grad_part.astype(jnp.bfloat16), "mp").astype(jnp.float32),
        lax.psum(depth_part.astype(jnp.bfloat16), "mp").astype(jnp.float32),
    )
    grad_inputs = grad_summed + grad_sum_one
    return (
        grad_inputs,
        (
            proj_grad[None],
            depth_total[None],
            kernel_grad[None],
            out_grad[None],
            gain_pair[None],
            bias_pair[None],
        ),
    )


def keep_valid(values, is_valid):
    return tuple((jnp.where(is_valid, member, 0.0) for member in values))


def on_device(
    hidden_in,
    segment_ids,
    cotangent,
    w_proj,
    w_depth,
    w_kernel,
    w_out,
    w_expand,
    shrink_weight,
    ln_gain,
    ln_bias,
):
    weights = (
        w_proj[0],
        w_depth[0].astype(jnp.float32),
        w_kernel[0],
        w_out[0],
        w_expand[0],
        shrink_weight[0],
        ln_gain[0].astype(jnp.float32),
        ln_bias[0].astype(jnp.float32),
    )
    section_index = lax.axis_index("section")
    outputs_low = jnp.zeros(hidden_in.shape, jnp.bfloat16)
    received = jnp.zeros((MB_ROWS,) + hidden_in.shape[1:], jnp.bfloat16)
    kept_ticks = []
    for tick_index in range(MICRO + 1):
        batch_step = tick_index - section_index
        row_start = jnp.clip(batch_step, 0, MICRO - 1) * MB_ROWS
        own_rows = min(tick_index, MICRO - 1) * MB_ROWS
        layer_in = jnp.where(
            section_index == 0, hidden_in[own_rows : own_rows + MB_ROWS], received
        ).astype(jnp.float32)
        segment = lax.dynamic_slice_in_dim(segment_ids, row_start, MB_ROWS, 0)
        out_low, kept_state = layer_forward(layer_in, segment, weights)
        is_valid = (batch_step >= 0) & (batch_step < MICRO)
        current = lax.dynamic_slice_in_dim(outputs_low, row_start, MB_ROWS, 0)
        outputs_low = lax.dynamic_update_slice_in_dim(
            outputs_low, jnp.where(is_valid, out_low, current), row_start, 0
        )
        received = from_behind(out_low, "section", 1)
        kept_ticks.append((segment, layer_in))
    grad_received = jnp.zeros((MB_ROWS,) + hidden_in.shape[1:], jnp.bfloat16)
    input_grads = jnp.zeros(hidden_in.shape, jnp.float32)
    ffn_totals = None
    mixer_totals = None
    for back_index in range(MICRO + 1):
        batch_step = MICRO - back_index - section_index
        row_start = jnp.clip(batch_step, 0, MICRO - 1) * MB_ROWS
        is_valid = (batch_step >= 0) & (batch_step < MICRO)
        own_rows = max(MICRO - 1 - back_index, 0) * MB_ROWS
        grad_out = jnp.where(
            section_index == 1,
            cotangent[own_rows : own_rows + MB_ROWS],
            grad_received.astype(jnp.float32),
        )
        segment, stored = kept_ticks[MICRO - back_index]
        kept_state = layer_forward(stored, segment, weights)[1]
        grad_first, ffn_grads, ffn_norm = ffn_backward(grad_out, kept_state, weights)
        ffn_part = keep_valid(ffn_grads, is_valid)
        ffn_totals = ffn_part if ffn_totals is None else jax.tree.map(jnp.add, ffn_totals, ffn_part)
        grad_inputs, mixer_grads = mixer_backward(
            grad_first, segment, kept_state, weights, ffn_norm
        )
        mixer_part = keep_valid(mixer_grads, is_valid)
        mixer_totals = (
            mixer_part if mixer_totals is None else jax.tree.map(jnp.add, mixer_totals, mixer_part)
        )
        current = lax.dynamic_slice_in_dim(input_grads, row_start, MB_ROWS, 0)
        input_grads = lax.dynamic_update_slice_in_dim(
            input_grads, jnp.where(is_valid, grad_inputs, current), row_start, 0
        )
        grad_received = from_behind(grad_inputs.astype(jnp.bfloat16), "section", -1)
    proj_sum, depth_sum, kernel_sum, out_sum, gain_sum, bias_sum = mixer_totals
    expand_sum, shrink_sum = ffn_totals
    proj_sum, depth_sum, kernel_sum, out_sum, expand_sum, shrink_sum, gain_sum, bias_sum = lax.psum(
        (proj_sum, depth_sum, kernel_sum, out_sum, expand_sum, shrink_sum, gain_sum, bias_sum), "dp"
    )
    return (
        outputs_low[None],
        input_grads[None],
        proj_sum,
        depth_sum,
        kernel_sum,
        out_sum,
        expand_sum,
        shrink_sum,
        gain_sum,
        bias_sum,
    )


def solution(mesh):
    in_specs = (
        P("dp", None, None),
        P("dp", None),
        P("dp", None, None),
        P("section", None, None, "mp"),
        P("section", None, None),
        P("section", "mp", None),
        P("section", None, "mp", None),
        P("section", "mp", None, None),
        P("section", "mp", None, None),
        P("section", None, None),
        P("section", None, None),
    )
    out_specs = (
        P("section", "dp", None, None),
        P("section", "dp", None, None),
        P("section", None, None, "mp"),
        P("section", None, None),
        P("section", "mp", None),
        P("section", None, "mp", None),
        P("section", "mp", None, None),
        P("section", "mp", None, None),
        P("section", None, None),
        P("section", None, None),
    )
    return jax.shard_map(
        on_device, mesh=mesh, in_specs=in_specs, out_specs=out_specs, check_vma=False
    )
```

profile of v0, /device:TPU:0, one launch (start us, length us, event | category | flops | bytes accessed | tf_op | source)
XLA Modules:
  0.0 1666.7 jit_solution(3359011371876524601)
XLA Ops:
  33.2 14.3 all-reduce.142.cloned.1.call-done
  57.1 51.0 %all-reduce.122.cloned.1.call-done = f32[1,512,768]{2,1,0:T(8,128)} async-done(((f32[1,512,768]{2,1,0:T(8,128)}), f32[1,512,768]{2,1,0:T(8,128)}) %all-reduce.122.cloned.1.call-update) | async-done | bytes 1572880 | tf_op jit(solution)/shard_map/psum | solution.py:161
  110.7 8.5 multiply_convert_fusion.4
  120.4 11.3 all-gather
  155.9 14.7 all-reduce.144.cloned.1.call-done
  179.4 51.7 %all-reduce.124.cloned.1.call-done = f32[1,512,768]{2,1,0:T(8,128)} async-done(((f32[1,512,768]{2,1,0:T(8,128)}), f32[1,512,768]{2,1,0:T(8,128)}) %all-reduce.124.cloned.1.call-update) | async-done | bytes 1572880 | tf_op jit(solution)/shard_map/psum | solution.py:161
  233.6 8.6 multiply_convert_fusion.3
  243.3 11.3 all-gather.1
  279.6 14.7 all-reduce.146.cloned.1.call-done
  303.3 51.7 %all-reduce.126.cloned.1.call-done = f32[1,512,768]{2,1,0:T(8,128)} async-done(((f32[1,512,768]{2,1,0:T(8,128)}), f32[1,512,768]{2,1,0:T(8,128)}) %all-reduce.126.cloned.1.call-update) | async-done | bytes 1572880 | tf_op jit(solution)/shard_map/psum | solution.py:161
  357.4 8.6 multiply_convert_fusion.2
  367.3 11.3 all-gather.2
  401.3 16.0 all-reduce.148.cloned.1.call-done
  421.6 51.7 %all-reduce.128.cloned.1.call-done = f32[1,512,768]{2,1,0:T(8,128)} async-done(((f32[1,512,768]{2,1,0:T(8,128)}), f32[1,512,768]{2,1,0:T(8,128)}) %all-reduce.128.cloned.1.call-update) | async-done | bytes 1572880 | tf_op jit(solution)/shard_map/psum | solution.py:161
  475.8 8.6 multiply_convert_fusion.1
  485.6 11.3 all-gather.3
  522.6 14.8 all-reduce.150.cloned.1.call-done
  551.9 47.3 %all-reduce.130.cloned.1.call-done = f32[1,512,768]{2,1,0:T(8,128)} async-done(((f32[1,512,768]{2,1,0:T(8,128)}), f32[1,512,768]{2,1,0:T(8,128)}) %all-reduce.130.cloned.1.call-update) | async-done | bytes 1572880 | tf_op jit(solution)/shard_map/psum | solution.py:161
  601.8 7.2 multiply_convert_fusion
  610.2 11.5 all-gather.4
  627.5 10.5 all-gather.5
  649.2 7.0 fusion.329
  656.2 7.1 fusion.293
  681.2 10.9 fusion.208
  701.4 32.6 %all-reduce.132.cloned.1.call-done = bf16[1,512,768]{2,1,0:T(8,128)(2,1)} async-done(((bf16[1,512,768]{2,1,0:T(8,128)(2,1)}), bf16[1,512,768]{2,1,0:T(8,128)(2,1)}) %all-reduce.132.cloned.1.call-update) | async-done | bytes 786448 | tf_op jit(solution)/shard_map/psum | solution.py:380
  772.1 12.0 all-gather.6
  795.3 7.1 fusion.332
  802.4 7.2 fusion.287
  827.8 11.4 fusion.199
  873.0 8.0 all-reduce.134.cloned.1.call-done
  900.8 12.7 all-gather.7
  924.6 7.0 fusion.335
  931.6 7.1 fusion.281
  978.2 25.0 %all-reduce.136.cloned.1.call-done = bf16[1,512,768]{2,1,0:T(8,128)(2,1)} async-done(((bf16[1,512,768]{2,1,0:T(8,128)(2,1)}), bf16[1,512,768]{2,1,0:T(8,128)(2,1)}) %all-reduce.136.cloned.1.call-update) | async-done | bytes 786448 | tf_op jit(solution)/shard_map/psum | solution.py:380
  1025.7 13.0 all-gather.8
  1049.8 7.2 fusion.338
  1056.9 7.1 fusion.275
  1113.4 15.3 all-reduce.138.cloned.1.call-done
  1153.1 12.7 all-gather.9
  1171.2 7.2 fusion.269
  1178.4 7.2 fusion.341
  1212.7 6.1 select_bitcast_fusion
  1232.3 6.3 fusion.153
  1239.3 11.1 all-reduce.156.cloned.1.call-done
  1267.7 6.2 copy.481
  1273.9 52.3 %all-reduce.152.cloned.1.call-done = (f32[1,9,768]{2,0,1:T(1,128)}, f32[1,192,54]{1,2,0:T(8,128)}, f32[1,2,768]{2,1,0:T(2,128)}, f32[1,2,768]{2,1,0:T(2,128)}) async-done(((f32[1,9,768]{2,0,1:T(1,128)}, f32[1,192,54]{1,2,0:T(8,128)}, f32[1,2,768]{2,1,0:T(2,128)}, f32[1,2,768]{2,1,0:T(2,128)}), (f32[1,9,768]{2,0,1:T(1,128)}, f32[1,192,54]{1,2,0:T(8,128)}, f32[1,2,768]{2,1,0:T(2,128)}, ...) | async-done | bytes 81424 | tf_op jit(solution)/shard_map/psum | solution.py:477
  1327.8 34.1 %all-reduce.140.cloned.1.call-done = bf16[1,512,768]{2,1,0:T(8,128)(2,1)} async-done(((bf16[1,512,768]{2,1,0:T(8,128)(2,1)}), bf16[1,512,768]{2,1,0:T(8,128)(2,1)}) %all-reduce.140.cloned.1.call-update) | async-done | bytes 786448 | tf_op jit(solution)/shard_map/psum | solution.py:380
  1364.9 283.7 %all-reduce.154.cloned.1.call-done = (f32[1,5,768,192]{2,3,1,0:T(8,128)}, f32[1,2,192,768]{3,2,1,0:T(8,128)}, f32[1,1,384,1536]{3,2,1,0:T(8,128)}, f32[1,1,1536,384]{3,2,1,0:T(8,128)}) async-done(((f32[1,5,768,192]{2,3,1,0:T(8,128)}, f32[1,2,192,768]{3,2,1,0:T(8,128)}, f32[1,1,384,1536]{3,2,1,0:T(8,128)}, f32[1,1,1536,384]{3,2,1,0:T(8,128)}), (f32[1,5,768,192]{2,3,1,0:T(8,128)}, ...) | async-done | bytes 8847376 | tf_op jit(solution)/shard_map/psum | solution.py:477
  (1864 shorter events, 581.4 us)
Async XLA Ops:
  7.2 103.5 %copy-start = (bf16[1,1,384,1536]{3,2,1,0:T(8,128)(2,1)S(1)}, bf16[1,1,384,1536]{3,2,1,0:T(8,128)(2,1)}, u32[]{:S(2)}) copy-start(bf16[1,1,384,1536]{3,2,1,0:T(8,128)(2,1)} %param.18) | copy-start | bytes 3538948
  7.2 40.3 %all-reduce.142.cloned.1.call-start = ((), (), s32[]{:S(2)}) async-start(), calls=%async_computation.10 | async-start | bytes 221184
  8.9 40.0 %copy-start.428 = (pred[512]{0:T(512)(128)(4,1)}, pred[512]{0:T(512)(128)(4,1)S(1)}, u32[]{:S(2)}) copy-start(pred[512]{0:T(512)(128)(4,1)S(1)} %get-tuple-element.225) | copy-start | bytes 1540
  23.3 84.9 %all-reduce.122.cloned.1.call-start = ((), (), s32[]{:S(2)}) async-start(), calls=%async_computation | async-start | bytes 3145728 | tf_op jit(solution)/shard_map/psum | solution.py:161
  30.0 23.5 %copy-start.1 = (bf16[1,2,192,768]{3,2,1,0:T(8,128)(2,1)S(1)}, bf16[1,2,192,768]{3,2,1,0:T(8,128)(2,1)}, u32[]{:S(2)}) copy-start(bf16[1,2,192,768]{3,2,1,0:T(8,128)(2,1)} %param.17) | copy-start | bytes 1769476
  56.4 114.2 %all-reduce.144.cloned.1.call-start = ((), (), s32[]{:S(2)}) async-start(), calls=%async_computation.11 | async-start | bytes 221184
  110.0 21.7 %copy-start.6 = (f32[1,512,768]{2,1,0:T(8,128)}, f32[1,512,768]{2,1,0:T(8,128)S(1)}, u32[]{:S(2)}) copy-start(f32[1,512,768]{2,1,0:T(8,128)S(1)} %get-tuple-element.303) | copy-start | bytes 4718596
  110.0 21.7 %copy-start.279 = (f32[512]{0:T(512)}, f32[512]{0:T(512)S(1)}, u32[]{:S(2)}) copy-start(f32[512]{0:T(512)S(1)} %broadcast_multiply_fusion.29) | copy-start | bytes 6148
  134.6 3.2 collective-permute-start
  149.1 82.0 %all-reduce.124.cloned.1.call-start = ((), (), s32[]{:S(2)}) async-start(), calls=%async_computation.1 | async-start | bytes 3145728 | tf_op jit(solution)/shard_map/psum | solution.py:161
  179.3 115.0 %all-reduce.146.cloned.1.call-start = ((), (), s32[]{:S(2)}) async-start(), calls=%async_computation.12 | async-start | bytes 221184
  232.9 21.8 %copy-start.2 = (f32[1,512,768]{2,1,0:T(8,128)}, f32[1,512,768]{2,1,0:T(8,128)S(1)}, u32[]{:S(2)}) copy-start(f32[1,512,768]{2,1,0:T(8,128)S(1)} %get-tuple-element.291) | copy-start | bytes 4718596
  232.9 21.7 %copy-start.281 = (f32[512]{0:T(512)}, f32[512]{0:T(512)S(1)}, u32[]{:S(2)}) copy-start(f32[512]{0:T(512)S(1)} %broadcast_multiply_fusion.27) | copy-start | bytes 6148
  258.3 3.2 collective-permute-start.1
  272.8 82.1 %all-reduce.126.cloned.1.call-start = ((), (), s32[]{:S(2)}) async-start(), calls=%async_computation.2 | async-start | bytes 3145728 | tf_op jit(solution)/shard_map/psum | solution.py:161
  303.2 114.1 %all-reduce.148.cloned.1.call-start = ((), (), s32[]{:S(2)}) async-start(), calls=%async_computation.13 | async-start | bytes 221184
  356.8 21.9 %copy-start.4 = (f32[1,512,768]{2,1,0:T(8,128)}, f32[1,512,768]{2,1,0:T(8,128)S(1)}, u32[]{:S(2)}) copy-start(f32[1,512,768]{2,1,0:T(8,128)S(1)} %get-tuple-element.279) | copy-start | bytes 4718596
  356.8 21.9 %copy-start.283 = (f32[512]{0:T(512)}, f32[512]{0:T(512)S(1)}, u32[]{:S(2)}) copy-start(f32[512]{0:T(512)S(1)} %broadcast_multiply_fusion.25) | copy-start | bytes 6148
  357.1 21.5 %copy-start.396 = (f32[512]{0:T(512)}, f32[512]{0:T(512)S(1)}, u32[]{:S(2)}) copy-start(f32[512]{0:T(512)S(1)} %add_rsqrt_fusion.5) | copy-start | bytes 6148
  382.3 3.2 collective-permute-start.2
  383.9 34.8 %copy-start.486 = (pred[512]{0:T(512)(128)(4,1)}, pred[512]{0:T(512)(128)(4,1)S(1)}, u32[]{:S(2)}) copy-start(pred[512]{0:T(512)(128)(4,1)S(1)} %get-tuple-element.201) | copy-start | bytes 1540
  383.9 34.8 %copy-start.488 = (pred[512]{0:T(512)(128)(4,1)}, pred[512]{0:T(512)(128)(4,1)S(1)}, u32[]{:S(2)}) copy-start(pred[512]{0:T(512)(128)(4,1)S(1)} %get-tuple-element.202) | copy-start | bytes 1540
  384.0 34.8 %copy-start.490 = (pred[512]{0:T(512)(128)(4,1)}, pred[512]{0:T(512)(128)(4,1)S(1)}, u32[]{:S(2)}) copy-start(pred[512]{0:T(512)(128)(4,1)S(1)} %get-tuple-element.203) | copy-start | bytes 1540
  384.0 34.8 %copy-start.493 = (pred[512]{0:T(512)(128)(4,1)}, pred[512]{0:T(512)(128)(4,1)S(1)}, u32[]{:S(2)}) copy-start(pred[512]{0:T(512)(128)(4,1)S(1)} %get-tuple-element.204) | copy-start | bytes 1540
  384.0 34.8 %copy-start.496 = (pred[512]{0:T(512)(128)(4,1)}, pred[512]{0:T(512)(128)(4,1)S(1)}, u32[]{:S(2)}) copy-start(pred[512]{0:T(512)(128)(4,1)S(1)} %get-tuple-element.205) | copy-start | bytes 1540
  384.0 34.8 %copy-start.499 = (pred[512]{0:T(512)(128)(4,1)}, pred[512]{0:T(512)(128)(4,1)S(1)}, u32[]{:S(2)}) copy-start(pred[512]{0:T(512)(128)(4,1)S(1)} %get-tuple-element.206) | copy-start | bytes 1540
  384.0 34.8 %copy-start.502 = (pred[512]{0:T(512)(128)(4,1)}, pred[512]{0:T(512)(128)(4,1)S(1)}, u32[]{:S(2)}) copy-start(pred[512]{0:T(512)(128)(4,1)S(1)} %get-tuple-element.207) | copy-start | bytes 1540
  384.0 34.8 %copy-start.554 = (pred[512]{0:T(512)(128)(4,1)}, pred[512]{0:T(512)(128)(4,1)S(1)}, u32[]{:S(2)}) copy-start(pred[512]{0:T(512)(128)(4,1)S(1)} %get-tuple-element.208) | copy-start | bytes 1540
  395.8 77.5 %all-reduce.128.cloned.1.call-start = ((), (), s32[]{:S(2)}) async-start(), calls=%async_computation.3 | async-start | bytes 3145728 | tf_op jit(solution)/shard_map/psum | solution.py:161
  421.6 115.7 %all-reduce.150.cloned.1.call-start = ((), (), s32[]{:S(2)}) async-start(), calls=%async_computation.14 | async-start | bytes 221184
  475.1 21.8 %copy-start.285 = (f32[512]{0:T(512)}, f32[512]{0:T(512)S(1)}, u32[]{:S(2)}) copy-start(f32[512]{0:T(512)S(1)} %broadcast_multiply_fusion.23) | copy-start | bytes 6148
  500.5 3.2 collective-permute-start.3
  515.8 83.3 %all-reduce.130.cloned.1.call-start = ((), (), s32[]{:S(2)}) async-start(), calls=%async_computation.4 | async-start | bytes 3145728 | tf_op jit(solution)/shard_map/psum | solution.py:161
  547.5 186.5 %all-reduce.132.cloned.1.call-start = ((), (), s32[]{:S(2)}) async-start(), calls=%async_computation.5 | async-start | bytes 1572864 | tf_op jit(solution)/shard_map/psum | solution.py:380
  599.2 23.5 %slice-start = ((s8[6291456]{0:T(1024)(128)(4,1)}), s8[4194304]{0:T(1024)(128)(4,1)S(1)}, s32[]{:S(2)}) async-start(s8[6291456]{0:T(1024)(128)(4,1)} %bitcast.1348), calls=%async_computation.18 | async-start | bytes 8388608
  699.4 181.6 %all-reduce.134.cloned.1.call-start = ((), (), s32[]{:S(2)}) async-start(), calls=%async_computation.6 | async-start | bytes 1572864 | tf_op jit(solution)/shard_map/psum | solution.py:380
  738.7 24.3 %collective-permute-start.4 = (bf16[1,512,768]{2,1,0:T(8,128)(2,1)}, bf16[1,512,768]{2,1,0:T(8,128)(2,1)}, u32[]{:S(2)}, u32[]{:S(2)}) collective-permute-start(bf16[1,512,768]{2,1,0:T(8,128)(2,1)} %get-tuple-element.312), channel_id=1, source_target_pairs={{16,0},{17,1},{18,2},{19,3},{20,4},{21,5},{22,6},{23,7},{24,8},{25... | collective-permute-start | bytes 2359304 | tf_op jit(solution)/shard_map/ppermute | solution.py:22
  802.4 23.7 %copy-start.89 = (bf16[1,192,54]{1,2,0:T(8,128)(2,1)S(1)}, bf16[1,192,54]{1,2,0:T(8,128)(2,1)}, u32[]{:S(2)}) copy-start(bf16[1,192,54]{1,2,0:T(8,128)(2,1)} %param.16) | copy-start | bytes 62212
  846.6 156.6 %all-reduce.136.cloned.1.call-start = ((), (), s32[]{:S(2)}) async-start(), calls=%async_computation.7 | async-start | bytes 1572864 | tf_op jit(solution)/shard_map/psum | solution.py:380
  884.7 7.2 collective-permute-start.5
  968.7 160.0 %all-reduce.138.cloned.1.call-start = ((), (), s32[]{:S(2)}) async-start(), calls=%async_computation.8 | async-start | bytes 1572864 | tf_op jit(solution)/shard_map/psum | solution.py:380
  1006.9 9.9 collective-permute-start.6
  1094.1 156.3 %all-reduce.156.cloned.1.call-start = ((), (), s32[]{:S(2)}) async-start(), calls=%async_computation.17 | async-start | bytes 245760 | tf_op jit(solution)/shard_map/psum | solution.py:381
  1132.3 6.2 collective-permute-start.7
  1228.5 97.8 %all-reduce.152.cloned.1.call-start = ((), (), s32[]{:S(2)}) async-start(), calls=%async_computation.15 | async-start | bytes 194560 | tf_op jit(solution)/shard_map/psum | solution.py:477
  1251.9 109.9 %all-reduce.140.cloned.1.call-start = ((), (), s32[]{:S(2)}) async-start(), calls=%async_computation.9 | async-start | bytes 1572864 | tf_op jit(solution)/shard_map/psum | solution.py:380
  1254.3 394.2 %all-reduce.154.cloned.1.call-start = ((), (), s32[]{:S(2)}) async-start(), calls=%async_computation.16 | async-start | bytes 17694720 | tf_op jit(solution)/shard_map/psum | solution.py:477
  1267.7 94.2 %copy-start.35 = (f32[1,512,768]{2,1,0:T(8,128)S(1)}, f32[1,512,768]{2,1,0:T(8,128)}, u32[]{:S(2)}) copy-start(f32[1,512,768]{2,1,0:T(8,128)} %copy-done.33) | copy-start | bytes 4718596
  (613 other events, 2867.6 us)
Sparse Core Ops, SparseCore 0:
  23.4 24.0 all-reduce.141
  56.5 51.5 all-reduce.121
  149.2 21.3 all-reduce.143
  179.5 51.5 all-reduce.123
  272.9 21.3 all-reduce.145
  303.3 51.5 all-reduce.125
  395.9 21.3 all-reduce.147
  421.7 51.5 all-reduce.127
  516.0 21.3 all-reduce.149
  547.6 51.5 all-reduce.129
  699.5 34.3 all-reduce.131
  846.6 34.3 all-reduce.133
  968.8 34.3 all-reduce.135
  1094.2 34.3 all-reduce.137
  1228.6 21.8 all-reduce.155
  1255.2 71.0 all-reduce.151
  1328.4 33.4 all-reduce.139
  1366.8 281.7 all-reduce.153
where the time goes:
time: 1680 us; the launch traced here: 1670 us
  waiting for transfers between devices  792 us (47%)
  matrix products  333 us (20%)
  other arithmetic  183 us (11%)
  local copies, waits for them, and re-layouts  178 us (11%)
  blocking collectives  143 us (9%)
  between operations  24.2 us (1%)
    psum x2, waiting for transfers between devices, on_device(): lax.psum((proj_sum, depth_sum, kernel_sum, out_sum, expand_sum, shrink_su...  336 us
    psum x5, waiting for transfers between devices, layer_forward(): mixer_out = lax.psum(mixer_part, 'mp')  253 us
    psum x5, waiting for transfers between devices, mixer_backward(): lax.psum(grad_part.astype(jnp.bfloat16), 'mp').astype(jnp.float32)  115 us
    unnamed x1367, local copies, waits for them, and re-layouts  91.4 us
    unnamed x23, waiting for transfers between devices  74.8 us
    all_gather x5, blocking collectives, ffn_backward(): lax.all_gather(grad_group_in.astype(jnp.bfloat16), 'mp', axis=2, tiled=True)  60.8 us
    all_gather x5, blocking collectives, layer_forward(): lax.all_gather(group_out.astype(jnp.bfloat16), 'mp', axis=2, tiled=True)  56.9 us
    dot_general x5, matrix products, layer_forward(): jnp.einsum('blc,cf->blf', group_low, w_expand[0], preferred_element_type=...  41.5 us
  transfers between devices with their start and end apart: 26, of which 22 were waited for; matrix products, arithmetic and copies ran while one was open for 10% of the time, Pallas kernels for 0%

commit v1 on v0

v1 whole, which is shorter than its diff:
```python
from functools import partial

import jax
import jax.numpy as jnp
from jax import lax
from jax.sharding import PartitionSpec as P

ATT_HEADS = 6
HEAD = 64
KSIZE = 9
EPS = 1e-05
FLOOR = -1000000000.0
BF = jnp.bfloat16
F32 = jnp.float32


def mm(a, b, dims):
    return lax.dot_general(a, b, (dims, ((), ())), preferred_element_type=F32)


def shift(values, by):
    length = values.shape[0]
    if by == 0:
        return values
    pad = ((max(-by, 0), max(by, 0)),) + ((0, 0),) * (values.ndim - 1)
    start = max(by, 0)
    return lax.slice_in_dim(jnp.pad(values, pad), start, start + length, axis=0)


def tap_masks(segment):
    half = KSIZE // 2
    padded = jnp.pad(segment, (half, half), constant_values=-1)
    length = segment.shape[0]
    return [
        (lax.slice_in_dim(padded, t, t + length) == segment)[:, None] for t in range(KSIZE)
    ]


def take(values, mask, t):
    return jnp.where(mask, shift(values, t - KSIZE // 2), 0.0)


def give(values, mask, t):
    return shift(jnp.where(mask, values, 0.0), KSIZE // 2 - t)


def norm_forward(summed, gain, bias):
    centered = summed - jnp.mean(summed, axis=-1, keepdims=True)
    inverse = lax.rsqrt(jnp.mean(centered * centered, axis=-1, keepdims=True) + EPS)
    normed = centered * inverse
    return normed * gain + bias, normed, inverse


def norm_backward(grad, normed, inverse, gain):
    u = grad * gain
    dz = inverse * (
        u
        - jnp.mean(u, axis=-1, keepdims=True)
        - normed * jnp.mean(u * normed, axis=-1, keepdims=True)
    )
    return dz, jnp.sum(grad * normed, axis=0), jnp.sum(grad, axis=0)


def heads_of(flat):
    return flat.reshape(flat.shape[0], ATT_HEADS, -1)


def layer_forward(x, segment, w):
    masks = tap_masks(segment)
    xb = x.astype(BF)
    proj = [mm(xb, w["proj"][p], ((1,), (0,))) for p in range(4)]
    depth = sum(take(x, masks[t], t) * w["depth"][t] for t in range(KSIZE))
    depth_low = depth.astype(BF)
    kc = mm(depth_low, w["proj"][4], ((1,), (0,)))
    prod_low = (kc * proj[0]).astype(BF)
    logits = mm(prod_low, w["kernel"], ((1,), (0,)))
    kern = jax.nn.softmax(heads_of(logits), axis=-1)
    cf = heads_of(proj[3])
    conv = sum(
        kern[..., t, None] * take(cf, masks[t][..., None], t) for t in range(KSIZE)
    )
    q, k, v = (heads_of(proj[p].astype(BF)) for p in range(3))
    scores = jnp.einsum("qhd,khd->hqk", q, k, preferred_element_type=F32) * HEAD**-0.5
    same = segment[:, None] == segment[None, :]
    probs = jax.nn.softmax(jnp.where(same, scores, FLOOR), axis=-1)
    ctx = jnp.einsum("hqk,khd->qhd", probs.astype(BF), v, preferred_element_type=F32)
    length = x.shape[0]
    cat = jnp.concatenate([ctx.reshape(length, -1), conv.reshape(length, -1)], axis=1).astype(BF)
    mixed = mm(cat, w["out"], ((1,), (0,)))
    y1, n0, s0 = norm_forward(mixed + x, w["gain"][0], w["bias"][0])
    groups, group_width, _ = w["expand"].shape
    grp = y1.astype(BF).reshape(length, groups, group_width)
    pre = jnp.einsum("lgc,gcf->glf", grp, w["expand"], preferred_element_type=F32)
    act = jax.nn.gelu(pre, approximate=False).astype(BF)
    ffn = jnp.einsum("glf,gfc->lgc", act, w["shrink"], preferred_element_type=F32)
    y2, n1, s1 = norm_forward(ffn.reshape(length, -1) + y1, w["gain"][1], w["bias"][1])
    kept = (x, proj, depth_low, kc, prod_low, kern, probs, cat, n0, s0, grp, pre, act, n1, s1)
    return y2.astype(BF), kept


def layer_backward(grad, segment, w, kept):
    x, proj, depth_low, kc, prod_low, kern, probs, cat, n0, s0, grp, pre, act, n1, s1 = kept
    length = x.shape[0]
    masks = tap_masks(segment)
    dz2, gain1, bias1 = norm_backward(grad, n1, s1, w["gain"][1])
    dffn = dz2.astype(BF).reshape(grp.shape)
    shrink_grad = jnp.einsum("glf,lgc->gfc", act, dffn, preferred_element_type=F32)
    dact = jnp.einsum("lgc,gfc->glf", dffn, w["shrink"], preferred_element_type=F32)
    dpre = jax.vjp(partial(jax.nn.gelu, approximate=False), pre)[1](dact)[0].astype(BF)
    expand_grad = jnp.einsum("lgc,glf->gcf", grp, dpre, preferred_element_type=F32)
    dgrp = jnp.einsum("glf,gcf->lgc", dpre, w["expand"], preferred_element_type=F32)
    dy1 = dz2 + dgrp.reshape(length, -1)
    dz1, gain0, bias0 = norm_backward(dy1, n0, s0, w["gain"][0])
    dmix = dz1.astype(BF)
    out_grad = mm(cat, dmix, ((0,), (0,)))
    dcat = mm(dmix, w["out"], ((1,), (1,))).astype(BF)
    half = dcat.shape[1] // 2
    dctx, dconv = heads_of(dcat[:, :half]), heads_of(dcat[:, half:]).astype(F32)
    q, k, v = (heads_of(proj[p].astype(BF)) for p in range(3))
    dprobs = jnp.einsum("qhd,khd->hqk", dctx, v, preferred_element_type=F32)
    row_dot = jnp.sum(probs * dprobs, axis=-1, keepdims=True)
    dscores = (probs * (dprobs - row_dot)).astype(BF)
    dq_att = jnp.einsum("hqk,khd->qhd", dscores, k, preferred_element_type=F32) * HEAD**-0.5
    dk = jnp.einsum("hqk,qhd->khd", dscores, q, preferred_element_type=F32) * HEAD**-0.5
    dv = jnp.einsum("hqk,qhd->khd", probs.astype(BF), dctx, preferred_element_type=F32)
    cf = heads_of(proj[3])
    dkern, dc = [], 0.0
    for t in range(KSIZE):
        mask = masks[t][..., None]
        dkern.append(jnp.sum(dconv * take(cf, mask, t), axis=-1))
        dc = dc + give(kern[..., t, None] * dconv, mask, t)
    dkern = jnp.stack(dkern, axis=-1)
    dlogits = kern * (dkern - jnp.sum(kern * dkern, axis=-1, keepdims=True))
    dlogits = dlogits.reshape(length, -1).astype(BF)
    kernel_grad = mm(prod_low, dlogits, ((0,), (0,)))
    dprod = mm(dlogits, w["kernel"], ((1,), (1,)))
    dkc = (dprod * proj[0]).astype(BF)
    dq = (dq_att.reshape(length, -1) + dprod * kc).astype(BF)
    ddepth = mm(dkc, w["proj"][4], ((1,), (1,)))
    depth_grad, dxd = [], 0.0
    for t in range(KSIZE):
        depth_grad.append(jnp.sum(ddepth * take(x, masks[t], t), axis=0))
        dxd = dxd + give(ddepth * w["depth"][t], masks[t], t)
    flat = lambda value: value.reshape(length, -1).astype(BF)
    dproj = [dq, flat(dk), flat(dv), flat(dc)]
    xb = x.astype(BF)
    proj_grad = jnp.stack(
        [mm(xb, one, ((0,), (0,))) for one in dproj] + [mm(depth_low, dkc, ((0,), (0,)))]
    )
    dx = dz1 + dxd + sum(mm(one, w["proj"][p], ((1,), (1,))) for p, one in enumerate(dproj))
    small = (
        jnp.stack(depth_grad),
        kernel_grad,
        jnp.stack([gain0, gain1]),
        jnp.stack([bias0, bias1]),
    )
    return dx, (proj_grad, out_grad, expand_grad, shrink_grad), small


def swap(value, axis):
    return lax.ppermute(value, axis, [(0, 1), (1, 0)])


def by_section(first, second):
    section = lax.axis_index("section")
    own = jnp.where(section == 0, first, second)
    other = swap(jnp.where(section == 0, second, first), "section")
    return jnp.where(section == 0, own, other), jnp.where(section == 0, other, own)


def on_device(
    hidden_in, segment_ids, cotangent, w_proj, w_depth, w_kernel, w_out, w_expand, shrink_weight,
    ln_gain, ln_bias,
):
    section, half = lax.axis_index("section"), lax.axis_index("mp")
    row = half * 2 + section

    def own_row(value):
        return lax.dynamic_index_in_dim(value, row, 0, keepdims=False)

    def whole(value, axis):
        if axis is not None:
            value = lax.all_gather(value, "mp", axis=axis, tiled=True)
        return lax.all_gather(value, "section", axis=0, tiled=True)

    proj = whole(w_proj, 3)
    out = whole(w_out, 2)
    expand = whole(w_expand, 1)
    shrink = whole(shrink_weight, 1)
    kernel = whole(w_kernel, 1)
    depth = whole(w_depth, None)
    gain = whole(ln_gain, None)
    bias = whole(ln_bias, None)
    weights = [
        dict(
            proj=proj[layer],
            out=out[layer].reshape(-1, out.shape[-1]),
            expand=expand[layer],
            shrink=shrink[layer],
            kernel=kernel[layer],
            depth=depth[layer].astype(F32),
            gain=gain[layer].astype(F32),
            bias=bias[layer].astype(F32),
        )
        for layer in range(2)
    ]
    segment = own_row(segment_ids)
    x0 = own_row(hidden_in).astype(F32)
    out0, kept0 = layer_forward(x0, segment, weights[0])
    out1, kept1 = layer_forward(out0.astype(F32), segment, weights[1])
    outputs = jnp.stack(by_section(out0, out1))
    outputs = lax.all_gather(outputs, "mp", axis=0, tiled=True)

    def reduced(grads):
        proj_grad, out_grad, expand_grad, shrink_grad = (g.astype(BF) for g in grads)
        width = proj_grad.shape[2] // 2
        parts = (
            (proj_grad, 1, 2),
            (out_grad.reshape(2, -1, out_grad.shape[-1]), 2, 1),
            (expand_grad, 2, 0),
            (shrink_grad, 2, 0),
        )
        done = []
        for value, piece_axis, half_axis in parts:
            value = lax.psum_scatter(
                value, "section", scatter_dimension=piece_axis, tiled=True
            )
            value = lax.psum_scatter(value, "mp", scatter_dimension=half_axis, tiled=True)
            done.append(lax.psum(value, "dp"))
        return done

    dx1, grads1, small1 = layer_backward(own_row(cotangent), segment, weights[1], kept1)
    big1 = reduced(grads1)
    g0 = dx1.astype(BF)
    dx0, grads0, small0 = layer_backward(g0.astype(F32), segment, weights[0], kept0)
    big0 = reduced(grads0)
    input_grads = jnp.stack(by_section(dx0.astype(BF), g0))
    input_grads = lax.all_gather(input_grads, "mp", axis=0, tiled=True).astype(F32)
    big = []
    for first, second, axis in zip(big0, big1, (1, 2, 2, 2)):
        big.append(jnp.concatenate(by_section(first, second), axis=axis)[None].astype(F32))
    small = lax.psum((small0, small1), ("section", "mp", "dp"))
    depth_grad, kernel_grad, gain_grad, bias_grad = (
        jnp.where(section == 0, a, b) for a, b in zip(*small)
    )
    kernel_half = kernel_grad.shape[0] // 2
    kernel_grad = lax.dynamic_slice_in_dim(kernel_grad, half * kernel_half, kernel_half, 0)
    return (
        outputs[None],
        input_grads[None],
        big[0],
        depth_grad[None],
        kernel_grad[None],
        big[1],
        big[2],
        big[3],
        gain_grad[None],
        bias_grad[None],
    )


def solution(mesh):
    in_specs = (
        P("dp", None, None),
        P("dp", None),
        P("dp", None, None),
        P("section", None, None, "mp"),
        P("section", None, None),
        P("section", "mp", None),
        P("section", None, "mp", None),
        P("section", "mp", None, None),
        P("section", "mp", None, None),
        P("section", None, None),
        P("section", None, None),
    )
    out_specs = (
        P("section", "dp", None, None),
        P("section", "dp", None, None),
        P("section", None, None, "mp"),
        P("section", None, None),
        P("section", "mp", None),
        P("section", None, "mp", None),
        P("section", "mp", None, None),
        P("section", "mp", None, None),
        P("section", None, None),
        P("section", None, None),
    )
    return jax.shard_map(
        on_device, mesh=mesh, in_specs=in_specs, out_specs=out_specs, check_vma=False
    )
```

time: 1680 us -> 1360 us (0.81)
  matrix products: 333 us -> 200 us
  blocking collectives: 143 us -> 12.6 us
  waiting for transfers between devices: 792 us -> 841 us
  other arithmetic: 183 us -> 135 us
  local copies, waits for them, and re-layouts: 178 us -> 147 us
    psum x13 -> x3, waiting for transfers between devices: 715 us -> 435 us  [the longest x2 259 us: on_device(): small = lax.psum((small0, small1), ('section', 'mp', 'dp'))]
    all_gather x0 -> x10, waiting for transfers between devices: none -> 240 us  [the longest x4 117 us: whole(): value = lax.all_gather(value, 'mp', axis=axis, tiled=True)]
    reduce_scatter x0 -> x12, waiting for transfers between devices: none -> 161 us  [the longest x6 120 us: reduced(): lax.psum_scatter(value, 'mp', scatter_dimension=half_axis, tiled=True)]
    dot_general x115 -> x62, matrix products: 327 us -> 186 us  [the longest x40 88.3 us: mm(): return lax.dot_general(a, b, (dims, ((), ())), preferred_element_type=F32)]
    all_gather x15 -> x5, blocking collectives: 143 us -> 12.6 us  [the longest x4 7.34 us: whole(): return lax.all_gather(value, 'section', axis=0, tiled=True)]
    unnamed x23 -> x33, waiting for transfers between devices: 74.8 us -> 3.69 us
    unnamed x1367 -> x580, local copies, waits for them, and re-layouts: 91.4 us -> 67.9 us
    reshape x5 -> x10, local copies, waits for them, and re-layouts: 0.91 us -> 22.5 us  [the longest x2 6.07 us: layer_backward(): dy1 = dz2 + dgrp.reshape(length, -1)]
  transfers between devices with their start and end apart: 26 -> 35, of which waited for: 22 -> 21; matrix products, arithmetic and copies ran while one was open for 10% -> 20% of each run, Pallas kernels for 0% -> 0%
where the time goes in v1:
time: 1360 us
  waiting for transfers between devices  841 us (62%)
  matrix products  200 us (15%)
  local copies, waits for them, and re-layouts  147 us (11%)
  other arithmetic  135 us (10%)
  between operations  18.1 us (1%)
    psum x2, waiting for transfers between devices, on_device(): small = lax.psum((small0, small1), ('section', 'mp', 'dp'))  259 us
    psum x1, waiting for transfers between devices, reduced(): done.append(lax.psum(value, 'dp'))  175 us
    reduce_scatter x6, waiting for transfers between devices, reduced(): lax.psum_scatter(value, 'mp', scatter_dimension=half_axis, tiled=True)  120 us
    all_gather x4, waiting for transfers between devices, whole(): value = lax.all_gather(value, 'mp', axis=axis, tiled=True)  117 us
    dot_general x40, matrix products, mm(): return lax.dot_general(a, b, (dims, ((), ())), preferred_element_type=F32)  88.3 us
    unnamed x580, local copies, waits for them, and re-layouts  67.9 us
    all_gather x1, waiting for transfers between devices, on_device(): outputs = lax.all_gather(outputs, 'mp', axis=0, tiled=True)  47.2 us
    all_gather x1, waiting for transfers between devices, on_device(): lax.all_gather(input_grads, 'mp', axis=0, tiled=True).astype(F32)  47.1 us
  transfers between devices with their start and end apart: 35, of which 21 were waited for; matrix products, arithmetic and copies ran while one was open for 20% of the time, Pallas kernels for 0%

profile of v1, /device:TPU:0, one launch (start us, length us, event | category | flops | bytes accessed | tf_op | source)
XLA Modules:
  0.0 1357.4 jit_solution(17859673527178033011)
XLA Ops:
  10.0 25.0 %all-gather.15.cloned.1.call-done = bf16[1,2,384,768]{3,2,1,0:T(8,128)(2,1)} async-done(((bf16[1,2,192,768]{3,2,1,0:T(8,128)(2,1)}), bf16[1,2,384,768]{3,2,1,0:T(8,128)(2,1)}) %all-gather.15.cloned.1.call-update) | async-done | bytes 1179664 | tf_op jit(solution)/shard_map/all_gather | solution.py:183
  35.1 44.2 %all-gather.11.cloned.1.call-done = bf16[1,5,768,384]{2,3,1,0:T(8,128)(2,1)} async-done(((bf16[1,5,768,192]{2,3,1,0:T(8,128)(2,1)}), bf16[1,5,768,384]{2,3,1,0:T(8,128)(2,1)}) %all-gather.11.cloned.1.call-update) | async-done | bytes 2949136 | tf_op jit(solution)/shard_map/all_gather | solution.py:183
  79.3 5.4 copy.147
  84.8 32.2 %all-gather.19.cloned.1.call-done = bf16[1,2,384,1536]{3,2,0,1:T(8,128)(2,1)} async-done(((bf16[1,1,384,1536]{3,2,0,1:T(8,128)(2,1)}), bf16[1,2,384,1536]{3,2,0,1:T(8,128)(2,1)}) %all-gather.19.cloned.1.call-update) | async-done | bytes 2359312 | tf_op jit(solution)/shard_map/all_gather | solution.py:183
  117.2 5.3 all_gather.48
  138.6 15.8 %all-gather.23.cloned.1.call-done = bf16[1,2,1536,384]{3,2,0,1:T(8,128)(2,1)} async-done(((bf16[1,1,1536,384]{3,2,0,1:T(8,128)(2,1)}), bf16[1,2,1536,384]{3,2,0,1:T(8,128)(2,1)}) %all-gather.23.cloned.1.call-update) | async-done | bytes 2359312 | tf_op jit(solution)/shard_map/all_gather | solution.py:183
  154.7 12.1 all-gather.17.cloned.1.call-done
  170.0 16.2 %all-gather.13.cloned.1.call-done = bf16[2,5,768,384]{3,2,1,0:T(8,128)(2,1)} async-done(((bf16[1,5,768,384]{3,2,1,0:T(8,128)(2,1)}), bf16[2,5,768,384]{3,2,1,0:T(8,128)(2,1)}) %all-gather.13.cloned.1.call-update) | async-done | bytes 5898256 | tf_op jit(solution)/shard_map/all_gather | solution.py:184
  198.1 5.1 fusion.257
  214.3 6.0 fusion.88
  222.9 15.3 %multiply_convert_fusion.3 = (bf16[2,512,1536]{2,1,0:T(8,128)(2,1)}, f32[2,512,1536]{2,1,0:T(8,128)}) fusion(f32[2,512,1536]{2,1,0:T(8,128)S(1)} %get-tuple-element.260, u8[512,1536]{1,0:T(8,128)(4,1)S(1)} %get-tuple-element.56, u8[512,1536]{1,0:T(8,128)(4,1)S(1)} %get-tuple-element.55), kind=kLoop, calls=%fused_computation.40 | loop fusion | flops 110100480 | bytes 17301504 | tf_op jit(solution)/shard_map/convert_element_type | solution.py:94
  238.2 4.0 fusion.31
  275.5 6.2 fusion.260
  295.1 5.8 fusion.89
  300.9 15.3 %multiply_convert_fusion.2 = (bf16[2,512,1536]{2,1,0:T(8,128)(2,1)S(1)}, f32[2,512,1536]{2,1,0:T(8,128)}) fusion(f32[2,512,1536]{2,1,0:T(8,128)S(1)} %get-tuple-element.268, u8[512,1536]{1,0:T(8,128)(4,1)S(1)} %get-tuple-element.54, u8[512,1536]{1,0:T(8,128)(4,1)S(1)} %get-tuple-element.53), kind=kLoop, calls=%fused_computation.25 | loop fusion | flops 110100480 | bytes 17301504 | tf_op jit(solution)/shard_map/convert_element_type | solution.py:94
  316.2 5.4 fusion.34
  336.0 8.9 add_convert_fusion.1
  344.9 5.4 fusion.32
  362.9 7.7 multiply_reduce_fusion.40
  374.3 4.8 fusion.126
  379.1 4.0 multiply_reduce_fusion.1
  431.9 5.3 fusion.76
  441.8 8.9 add_convert_fusion
  450.7 5.4 fusion.29
  470.1 4.0 multiply_reduce_fusion
  517.9 4.7 convolution_convert_fusion
  522.7 5.1 convolution_convert_fusion.2
  527.9 3.9 convolution_convert_fusion.1
  533.0 4.7 convolution_convert_fusion.3
  555.9 13.1 reduce-scatter.37.cloned.1.call-done
  569.1 14.0 %reduce-scatter.41.cloned.1.call-done = bf16[2,1536,192]{1,2,0:T(8,128)(2,1)} async-done(((bf16[2,1536,384]{1,2,0:T(8,128)(2,1)}), bf16[2,1536,192]{1,2,0:T(8,128)(2,1)}) %reduce-scatter.41.cloned.1.call-update) | async-done | bytes 1179664 | tf_op jit(solution)/shard_map/reduce_scatter | solution.py:225
  583.2 13.9 %reduce-scatter.33.cloned.1.call-done = bf16[2,384,768]{2,1,0:T(8,128)(2,1)} async-done(((bf16[2,384,1536]{2,1,0:T(8,128)(2,1)}), bf16[2,384,768]{2,1,0:T(8,128)(2,1)}) %reduce-scatter.33.cloned.1.call-update) | async-done | bytes 1179664 | tf_op jit(solution)/shard_map/reduce_scatter | solution.py:225
  611.6 6.8 multiply_select_fusion.8
  618.3 4.2 multiply_reduce_fusion.13
  648.5 5.0 broadcast_select_fusion.2
  664.5 5.9 reduce-scatter.31.cloned.1.call-done
  670.4 17.5 %reduce-scatter.29.cloned.1.call-done = bf16[2,192,384]{2,1,0:T(8,128)(2,1)} async-done(((bf16[2,384,384]{2,1,0:T(8,128)(2,1)}), bf16[2,192,384]{2,1,0:T(8,128)(2,1)}) %reduce-scatter.29.cloned.1.call-update) | async-done | bytes 294928 | tf_op jit(solution)/shard_map/reduce_scatter | solution.py:228
  687.9 24.1 %reduce-scatter.47.cloned.1.call-done = bf16[1,1536,192]{1,2,0:T(8,128)(2,1)} async-done(((bf16[2,1536,192]{1,2,0:T(8,128)(2,1)}), bf16[1,1536,192]{1,2,0:T(8,128)(2,1)}) %reduce-scatter.47.cloned.1.call-update) | async-done | bytes 589840 | tf_op jit(solution)/shard_map/reduce_scatter | solution.py:228
  712.0 24.1 %reduce-scatter.39.cloned.1.call-done = bf16[1,384,768]{2,1,0:T(8,128)(2,1)} async-done(((bf16[2,384,768]{2,1,0:T(8,128)(2,1)}), bf16[1,384,768]{2,1,0:T(8,128)(2,1)}) %reduce-scatter.39.cloned.1.call-update) | async-done | bytes 589840 | tf_op jit(solution)/shard_map/reduce_scatter | solution.py:228
  736.1 24.1 %reduce-scatter.43.cloned.1.call-done = bf16[1,1536,192]{1,2,0:T(8,128)(2,1)} async-done(((bf16[2,1536,192]{1,2,0:T(8,128)(2,1)}), bf16[1,1536,192]{1,2,0:T(8,128)(2,1)}) %reduce-scatter.43.cloned.1.call-update) | async-done | bytes 589840 | tf_op jit(solution)/shard_map/reduce_scatter | solution.py:228
  760.3 24.0 %reduce-scatter.35.cloned.1.call-done = bf16[1,384,768]{2,1,0:T(8,128)(2,1)} async-done(((bf16[2,384,768]{2,1,0:T(8,128)(2,1)}), bf16[1,384,768]{2,1,0:T(8,128)(2,1)}) %reduce-scatter.35.cloned.1.call-update) | async-done | bytes 589840 | tf_op jit(solution)/shard_map/reduce_scatter | solution.py:228
  784.3 134.0 %all-reduce.72.cloned.1.call-done = (f32[9,768]{1,0:T(8,128)}, f32[9,768]{1,0:T(8,128)}, f32[2,768]{1,0:T(2,128)}, f32[2,768]{1,0:T(2,128)}, f32[2,768]{1,0:T(2,128)}, /*index=5*/f32[2,768]{1,0:T(2,128)}) async-done(((f32[9,768]{1,0:T(8,128)}, f32[9,768]{1,0:T(8,128)}, f32[2,768]{1,0:T(2,128)}, f32[2,768]{1,0:T(2,128)}, f32[2,768]{1,0:T(2,128)}, /*index=5*/f32[2,768]{1,0:T(2,128)}), (f32[9,768]{1,0:T(8,128)}, ...) | async-done | bytes 79888 | tf_op jit(solution)/shard_map/psum | solution.py:242
  922.3 125.4 %all-reduce.74.cloned.1.call-done = (f32[384,54]{0,1:T(8,128)}, f32[384,54]{0,1:T(8,128)}) async-done(((f32[384,54]{0,1:T(8,128)}, f32[384,54]{0,1:T(8,128)}), (f32[384,54]{0,1:T(8,128)}, f32[384,54]{0,1:T(8,128)})) %all-reduce.74.cloned.1.call-update) | async-done | bytes 165904 | tf_op jit(solution)/shard_map/psum | solution.py:242
  1049.4 47.2 %all-gather.27.cloned.1.call-done = bf16[4,512,768]{2,1,0:T(8,128)(2,1)} async-done(((bf16[2,512,768]{2,1,0:T(8,128)(2,1)}), bf16[4,512,768]{2,1,0:T(8,128)(2,1)}) %all-gather.27.cloned.1.call-update) | async-done | bytes 3145744 | tf_op jit(solution)/shard_map/all_gather | solution.py:212
  1096.6 47.1 %all-gather.29.cloned.1.call-done = bf16[4,512,768]{2,1,0:T(8,128)(2,1)} async-done(((bf16[2,512,768]{2,1,0:T(8,128)(2,1)}), bf16[4,512,768]{2,1,0:T(8,128)(2,1)}) %all-gather.29.cloned.1.call-update) | async-done | bytes 3145744 | tf_op jit(solution)/shard_map/all_gather | solution.py:238
  1143.6 5.1 bitcast_convert_fusion
  1148.7 175.1 %all-reduce.76.cloned.1.call-done = (bf16[5,384,192]{2,1,0:T(8,128)(2,1)}, bf16[5,384,192]{2,1,0:T(8,128)(2,1)}, bf16[2,192,384]{2,1,0:T(8,128)(2,1)}, bf16[2,19...) async-done(((bf16[5,384,192]{2,1,0:T(8,128)(2,1)}, ...) | async-done | bytes 4423696 | tf_op jit(solution)/shard_map/psum | solution.py:229
  1343.7 5.2 copy.195
  (881 shorter events, 331.6 us)
Async XLA Ops:
  7.2 124.1 %copy-start = (s32[4,512]{1,0:T(4,128)S(1)}, s32[4,512]{1,0:T(4,128)}, u32[]{:S(2)}) copy-start(s32[4,512]{1,0:T(4,128)} %param.12) | copy-start | bytes 24580
  7.2 27.9 %all-gather.15.cloned.1.call-start = ((), (), s32[]{:S(2)}) async-start(), calls=%async_computation.18 | async-start | bytes 1769472 | tf_op jit(solution)/shard_map/all_gather | solution.py:183
  7.9 71.4 %all-gather.11.cloned.1.call-start = ((), (), s32[]{:S(2)}) async-start(), calls=%async_computation.16 | async-start | bytes 4423680 | tf_op jit(solution)/shard_map/all_gather | solution.py:183
  8.7 108.3 %all-gather.19.cloned.1.call-start = ((), (), s32[]{:S(2)}) async-start(), calls=%async_computation.20 | async-start | bytes 3538944 | tf_op jit(solution)/shard_map/all_gather | solution.py:183
  9.4 145.0 %all-gather.23.cloned.1.call-start = ((), (), s32[]{:S(2)}) async-start(), calls=%async_computation.22 | async-start | bytes 3538944 | tf_op jit(solution)/shard_map/all_gather | solution.py:183
  10.0 156.8 %all-gather.17.cloned.1.call-start = ((), (), s32[]{:S(2)}) async-start(), calls=%async_computation.19 | async-start | bytes 3538944 | tf_op jit(solution)/shard_map/all_gather | solution.py:184
  35.1 151.1 %all-gather.13.cloned.1.call-start = ((), (), s32[]{:S(2)}) async-start(), calls=%async_computation.17 | async-start | bytes 8847360 | tf_op jit(solution)/shard_map/all_gather | solution.py:184
  84.7 32.3 %copy-start.235 = (bf16[1,192,54]{1,2,0:T(8,128)(2,1)S(1)}, bf16[1,192,54]{1,2,0:T(8,128)(2,1)}, u32[]{:S(2)}) copy-start(bf16[1,192,54]{1,2,0:T(8,128)(2,1)} %param.16) | copy-start | bytes 62212
  84.7 129.5 %all-gather.21.cloned.1.call-start = ((), (), s32[]{:S(2)}) async-start(), calls=%async_computation.21 | async-start | bytes 7077888 | tf_op jit(solution)/shard_map/all_gather | solution.py:184
  117.0 121.2 %all-gather.25.cloned.1.call-start = ((), (), s32[]{:S(2)}) async-start(), calls=%async_computation.23 | async-start | bytes 7077888 | tf_op jit(solution)/shard_map/all_gather | solution.py:184
  133.3 114.5 %copy-start.203 = (f32[768]{0:T(1024)}, f32[768]{0:T(1024)S(1)}, u32[]{:S(2)}) copy-start(f32[768]{0:T(1024)S(1)} %get-tuple-element.105) | copy-start | bytes 9220
  134.7 113.1 %copy-start.145 = (pred[512]{0:T(512)(128)(4,1)}, pred[512]{0:T(512)(128)(4,1)S(1)}, u32[]{:S(2)}) copy-start(pred[512]{0:T(512)(128)(4,1)S(1)} %get-tuple-element.246) | copy-start | bytes 1540
  134.7 113.1 %copy-start.148 = (pred[512]{0:T(512)(128)(4,1)}, pred[512]{0:T(512)(128)(4,1)S(1)}, u32[]{:S(2)}) copy-start(pred[512]{0:T(512)(128)(4,1)S(1)} %get-tuple-element.247) | copy-start | bytes 1540
  134.7 113.1 %copy-start.153 = (pred[512]{0:T(512)(128)(4,1)}, pred[512]{0:T(512)(128)(4,1)S(1)}, u32[]{:S(2)}) copy-start(pred[512]{0:T(512)(128)(4,1)S(1)} %get-tuple-element.248) | copy-start | bytes 1540
  134.7 113.1 %copy-start.158 = (pred[512]{0:T(512)(128)(4,1)}, pred[512]{0:T(512)(128)(4,1)S(1)}, u32[]{:S(2)}) copy-start(pred[512]{0:T(512)(128)(4,1)S(1)} %get-tuple-element.249) | copy-start | bytes 1540
  134.7 113.1 %copy-start.165 = (pred[512]{0:T(512)(128)(4,1)}, pred[512]{0:T(512)(128)(4,1)S(1)}, u32[]{:S(2)}) copy-start(pred[512]{0:T(512)(128)(4,1)S(1)} %get-tuple-element.250) | copy-start | bytes 1540
  134.7 113.1 %copy-start.172 = (pred[512]{0:T(512)(128)(4,1)}, pred[512]{0:T(512)(128)(4,1)S(1)}, u32[]{:S(2)}) copy-start(pred[512]{0:T(512)(128)(4,1)S(1)} %get-tuple-element.251) | copy-start | bytes 1540
  134.7 113.1 %copy-start.196 = (pred[512]{0:T(512)(128)(4,1)}, pred[512]{0:T(512)(128)(4,1)S(1)}, u32[]{:S(2)}) copy-start(pred[512]{0:T(512)(128)(4,1)S(1)} %get-tuple-element.252) | copy-start | bytes 1540
  135.0 63.1 %copy-start.109 = (pred[512,512]{0,1:T(8,128)(4,1)}, pred[512,512]{0,1:T(8,128)(4,1)S(1)}, u32[]{:S(2)}) copy-start(pred[512,512]{0,1:T(8,128)(4,1)S(1)} %broadcast_compare_fusion) | copy-start | bytes 786436
  138.6 51.9 %copy-start.44 = (bf16[512,768]{1,0:T(8,128)(2,1)}, bf16[512,768]{1,0:T(8,128)(2,1)S(1)}, u32[]{:S(2)}) copy-start(bf16[512,768]{1,0:T(8,128)(2,1)S(1)} %add_convert_fusion.5) | copy-start | bytes 2359300
  154.5 383.3 %reduce-scatter.27.cloned.1.call-start = ((), (), s32[]{:S(2)}) async-start(), calls=%async_computation.27 | async-start | bytes 4423680 | tf_op jit(solution)/shard_map/reduce_scatter | solution.py:225
  212.9 30.9 %copy-start.179 = (f32[512]{0:T(512)}, f32[512]{0:T(512)S(1)}, u32[]{:S(2)}) copy-start(f32[512]{0:T(512)S(1)} %broadcast_multiply_fusion.11) | copy-start | bytes 6148
  419.1 123.3 %reduce-scatter.25.cloned.1.call-start = ((), (), s32[]{:S(2)}) async-start(), calls=%async_computation.26 | async-start | bytes 4423680 | tf_op jit(solution)/shard_map/reduce_scatter | solution.py:225
  504.2 42.8 %reduce-scatter.55.cloned.1.call-start = ((), (), s32[]{:S(2)}) async-start(), calls=%async_computation.41 | async-start | bytes 1769472
  513.3 37.6 %reduce-scatter.53.cloned.1.call-start = ((), (), s32[]{:S(2)}) async-start(), calls=%async_computation.40 | async-start | bytes 1769472
  517.9 37.3 %reduce-scatter.45.cloned.1.call-start = ((), (), s32[]{:S(2)}) async-start(), calls=%async_computation.36 | async-start | bytes 3538944 | tf_op jit(solution)/shard_map/reduce_scatter | solution.py:225
  522.7 46.4 %reduce-scatter.37.cloned.1.call-start = ((), (), s32[]{:S(2)}) async-start(), calls=%async_computation.32 | async-start | bytes 3538944 | tf_op jit(solution)/shard_map/reduce_scatter | solution.py:225
  527.8 55.3 %reduce-scatter.41.cloned.1.call-start = ((), (), s32[]{:S(2)}) async-start(), calls=%async_computation.34 | async-start | bytes 3538944 | tf_op jit(solution)/shard_map/reduce_scatter | solution.py:225
  531.8 65.2 %reduce-scatter.33.cloned.1.call-start = ((), (), s32[]{:S(2)}) async-start(), calls=%async_computation.30 | async-start | bytes 3538944 | tf_op jit(solution)/shard_map/reduce_scatter | solution.py:225
  537.7 119.7 %reduce-scatter.51.cloned.1.call-start = ((), (), s32[]{:S(2)}) async-start(), calls=%async_computation.39 | async-start | bytes 2211840
  542.3 118.7 %reduce-scatter.49.cloned.1.call-start = ((), (), s32[]{:S(2)}) async-start(), calls=%async_computation.38 | async-start | bytes 2211840
  546.9 123.5 %reduce-scatter.31.cloned.1.call-start = ((), (), s32[]{:S(2)}) async-start(), calls=%async_computation.29 | async-start | bytes 884736 | tf_op jit(solution)/shard_map/reduce_scatter | solution.py:228
  550.8 137.1 %reduce-scatter.29.cloned.1.call-start = ((), (), s32[]{:S(2)}) async-start(), calls=%async_computation.28 | async-start | bytes 884736 | tf_op jit(solution)/shard_map/reduce_scatter | solution.py:228
  555.1 156.9 %reduce-scatter.47.cloned.1.call-start = ((), (), s32[]{:S(2)}) async-start(), calls=%async_computation.37 | async-start | bytes 1769472 | tf_op jit(solution)/shard_map/reduce_scatter | solution.py:228
  555.9 180.3 %reduce-scatter.39.cloned.1.call-start = ((), (), s32[]{:S(2)}) async-start(), calls=%async_computation.33 | async-start | bytes 1769472 | tf_op jit(solution)/shard_map/reduce_scatter | solution.py:228
  569.1 191.2 %reduce-scatter.43.cloned.1.call-start = ((), (), s32[]{:S(2)}) async-start(), calls=%async_computation.35 | async-start | bytes 1769472 | tf_op jit(solution)/shard_map/reduce_scatter | solution.py:228
  583.2 201.1 %reduce-scatter.35.cloned.1.call-start = ((), (), s32[]{:S(2)}) async-start(), calls=%async_computation.31 | async-start | bytes 1769472 | tf_op jit(solution)/shard_map/reduce_scatter | solution.py:228
  597.1 321.1 %all-reduce.72.cloned.1.call-start = ((), (), s32[]{:S(2)}) async-start(), calls=%async_computation.42 | async-start | bytes 245760 | tf_op jit(solution)/shard_map/psum | solution.py:242
  602.2 37.0 %collective-permute-start = (bf16[512,768]{1,0:T(8,128)(2,1)}, bf16[512,768]{1,0:T(8,128)(2,1)}, u32[]{:S(2)}, u32[]{:S(2)}) collective-permute-start(bf16[512,768]{1,0:T(8,128)(2,1)} %get-tuple-element.151), channel_id=1, source_target_pairs={{0,16},{16,0},{1,17},{17,1},{2,18},{18,2},{3,19},{19,3},{4,20},{20... | collective-permute-start | bytes 2359304 | tf_op jit(solution)/shard_map/ppermute | solution.py:161
  635.3 412.4 %all-reduce.74.cloned.1.call-start = ((), (), s32[]{:S(2)}) async-start(), calls=%async_computation.43 | async-start | bytes 344064 | tf_op jit(solution)/shard_map/psum | solution.py:242
  639.2 457.4 %all-gather.27.cloned.1.call-start = ((), (), s32[]{:S(2)}) async-start(), calls=%async_computation.24 | async-start | bytes 4718592 | tf_op jit(solution)/shard_map/all_gather | solution.py:212
  641.9 501.7 %all-gather.29.cloned.1.call-start = ((), (), s32[]{:S(2)}) async-start(), calls=%async_computation.25 | async-start | bytes 4718592 | tf_op jit(solution)/shard_map/all_gather | solution.py:238
  653.5 2.4 collective-permute-start.1
  657.3 666.6 %all-reduce.76.cloned.1.call-start = ((), (), s32[]{:S(2)}) async-start(), calls=%async_computation.44 | async-start | bytes 9830400 | tf_op jit(solution)/shard_map/psum | solution.py:229
  1325.0 5.7 collective-permute-start.3
  1327.2 5.7 collective-permute-start.5
  1328.5 7.8 collective-permute-start.4
  1330.2 9.1 collective-permute-start.2
  (258 other events, 1239.0 us)
Sparse Core Ops, SparseCore 0:
  9.5 25.4 all-gather.14
  36.6 42.6 all-gather.10
  80.9 36.0 all-gather.18
  118.3 36.0 all-gather.22
  155.8 10.9 all-gather.16
  168.8 17.3 all-gather.12
  187.7 15.5 all-gather.20
  204.9 15.5 all-gather.24
  419.2 11.8 reduce-scatter.26
  504.4 11.8 reduce-scatter.24
  518.5 9.7 reduce-scatter.54
  531.0 9.7 reduce-scatter.52
  543.7 11.3 reduce-scatter.44
  557.8 11.2 reduce-scatter.36
  571.7 11.3 reduce-scatter.40
  585.8 11.2 reduce-scatter.32
  599.2 26.3 reduce-scatter.50
  627.7 25.0 reduce-scatter.48
  655.0 15.3 reduce-scatter.30
  672.5 15.3 reduce-scatter.28
  690.2 21.8 reduce-scatter.46
  714.3 21.8 reduce-scatter.38
  738.4 21.8 reduce-scatter.42
  762.4 21.8 reduce-scatter.34
  791.8 126.3 all-reduce.71
  923.7 123.9 all-reduce.73
  1049.7 46.8 all-gather.26
  1098.7 44.8 all-gather.28
  1148.7 175.1 all-reduce.75
